TPU v7x, 128 devices: a whole 4x4x4 slice. The times are simulated.
128 devices in a mesh: blk: 64 (over z, y, x_hi, core), head: 2 (over x_lo).
Axes of the slice: x: 4 (x_hi: 2, x_lo: 2; x = x_hi * 2 + x_lo), y: 4, z: 4, core: 2. Of those that a mesh axis runs over, the one named last changes fastest.
Arguments:
- queries: bfloat16 [16384, 1024], P('blk', 'head'), may hold values from -216 to 216
- keys: bfloat16 [16384, 1024], P('blk', 'head'), may hold values from -6 to 6
- values: bfloat16 [16384, 1024], P('blk', 'head'), may hold values from -6 to 6
- group_table: int32 [64, 2], P('blk'), may hold values from 0 to 127, as said below
- doc_ids: int32 [16384], replicated, may hold values from 0 to 15, never falling along the last dimension, each value on 1 to 8192 neighbouring positions
Outputs:
- attended: bfloat16 [16384, 1024], P('blk', 'head')
Inputs may be any that keep to these rules, and one draw needn't show every extreme that they name: group_table[d, 1] = 127 - group_table[d, 0]; the first column holds each of 0 to 63 once. `doc_ids`: document numbers never fall along positions; a document holds at most 8192 positions.
All inputs are finite; a program needn't handle non-finite values.
Results may differ from a plain program's by a relative error of at most 0.0049.
Values may be sent and summed in bfloat16 or wider, within the bound.
A program may use at most 192 MiB of HBM per device.

v0:
```python
import math

import jax
import jax.numpy as jnp
from jax import lax
from jax.experimental import pallas as pl
from jax.experimental.pallas import tpu as pltpu
from jax.sharding import Mesh
from jax.sharding import PartitionSpec as P

HEAD_DIM = 128
GROUP = 128
GROUPS = 128
AXES = ("z", "y", "xh", "core", "head")
BLK = AXES[:4]
MESH = pl.DeviceIdType.MESH
K_ROWS = 2 * GROUP + 16
CHUNK = K_ROWS + 2 * GROUP
Q_AT, Q_ROWS = CHUNK, 2 * GROUP + 16
NEG = -1e30
MASKED = -3e38
FAR = 1 << 20
TILE = 4
COEF = math.log2(math.e) / math.sqrt(HEAD_DIM)


def place():
    return tuple(lax.axis_index(a) for a in AXES)


def remote(src, dst, send, recv, to):
    return pltpu.make_async_remote_copy(
        src_ref=src, dst_ref=dst, send_sem=send, recv_sem=recv, device_id=to, device_id_type=MESH
    )


def spread_kernel(
    q_hbm, k_hbm, v_hbm, table_hbm, doc_hbm, kv_out, q_out, start_out, src, q_in, v_in, docs, table, loc, snd, own, yp, ym, rl, dd, qr
):
    z, y, xh, c, hd = place()
    up, down, over = lax.rem(y + 1, 4), lax.rem(y + 3, 4), lax.rem(y + 2, 4)
    zs = [z, lax.rem(z + 1, 4), lax.rem(z + 2, 4), lax.rem(z + 3, 4)]
    to_up, to_down, to_core = (z, up, xh, c, hd), (z, down, xh, c, hd), (z, y, xh, 1 - c, hd)
    local = [
        pltpu.make_async_copy(table_hbm, table, loc.at[0]),
        pltpu.make_async_copy(v_hbm, v_in, loc.at[1]),
        pltpu.make_async_copy(q_hbm, q_in, loc.at[2]),
        pltpu.make_async_copy(doc_hbm, docs, loc.at[3]),
    ]
    for h in range(4):
        keys_of_head = k_hbm.at[:, pl.ds(h * HEAD_DIM, HEAD_DIM)]
        local.append(pltpu.make_async_copy(keys_of_head, src.at[h, pl.ds(0, 2 * GROUP)], loc.at[4 + h]))
    for copy in local:
        copy.start()
    partners = [(zs[dz], y, xh, c, hd) for dz in (1, 2, 3)]
    partners += [(zs[dz], y, 1 - xh, c, hd) for dz in range(4)] + [to_up, to_down, to_core]
    barrier = pltpu.get_barrier_semaphore()
    for to in partners:
        pl.semaphore_signal(barrier, inc=1, device_id=to, device_id_type=MESH)

    local[0].wait()
    first = table[0, 0].astype(jnp.float32)
    for h in range(4):
        header = jnp.full((16, HEAD_DIM), first, jnp.float32).astype(jnp.bfloat16)
        src[h, K_ROWS - 16 : K_ROWS, :] = header
        src[h, Q_AT + 2 * GROUP :, :] = header
    local[1].wait()
    for h in range(4):
        for s in range(2):
            rows, cols = slice(s * GROUP, (s + 1) * GROUP), slice(h * HEAD_DIM, (h + 1) * HEAD_DIM)
            src[h, K_ROWS + s * GROUP : K_ROWS + (s + 1) * GROUP, :] = v_in[rows, cols].T
    for copy in local[2:]:
        copy.wait()
    pl.semaphore_wait(barrier, len(partners))

    sent = []

    def start(src_ref, dst_ref, recv, to):
        copy = remote(src_ref, dst_ref, snd.at[len(sent)], recv, to)
        copy.start()
        sent.append(copy)

    def landed(dst_ref, recv):
        remote(dst_ref, dst_ref, snd.at[0], recv, to_core).wait_recv()

    span = (pl.ds(0, K_ROWS), pl.ds(K_ROWS, 2 * GROUP))

    def piece(zz, yy, cc, p):
        return kv_out.at[(zz * 4 + yy) * 2 + cc, span[p]]

    order = (0, 1, 3, 2)
    came = [zs[(4 - dz) % 4] for dz in order]

    def first_hop(s, p):
        mine = piece(came[s], y, c, p)
        here = src.at[z, span[p]]
        if s > 0:
            landed(mine, own.at[s, p])
            here = mine
        start(here, mine, yp.at[s, p], to_up)
        start(here, mine, ym.at[s, p], to_down)
        start(here, mine, dd.at[s, 0, p], to_core)

    def second_hop(s, p):
        below, above = piece(came[s], down, c, p), piece(came[s], up, c, p)
        landed(below, yp.at[s, p])
        if p == 0:
            start(below, below, rl.at[s, p], to_up)
        start(below, below, dd.at[s, 1, p], to_core)
        landed(above, ym.at[s, p])
        if p == 1:
            start(above, above, rl.at[s, p], to_down)
        start(above, above, dd.at[s, 2, p], to_core)

    def last_hop(s, p):
        across = piece(came[s], over, c, p)
        landed(across, rl.at[s, p])
        start(across, across, dd.at[s, 3, p], to_core)

    first_hop(0, 0)
    for s, p in ((1, 0), (2, 0), (1, 1), (2, 1), (3, 0), (3, 1)):
        dz = order[s]
        start(src.at[zs[dz], span[p]], piece(z, y, c, p), own.at[s, p], (zs[dz], y, xh, c, hd))
    first_hop(0, 1)
    kv_out[(z * 4 + y) * 2 + c] = src[z, 0:CHUNK]
    for h in range(4):
        for s in range(2):
            rows, cols = slice(s * GROUP, (s + 1) * GROUP), slice(h * HEAD_DIM, (h + 1) * HEAD_DIM)
            src[h, Q_AT + s * GROUP : Q_AT + (s + 1) * GROUP, :] = q_in[rows, cols].T
    held = docs[...]
    for d in range(16):
        counted = jnp.sum(jnp.where(held < d, 1, 0), axis=0, keepdims=True)
        start_out[d : d + 1, :] = jnp.broadcast_to(jnp.sum(counted, axis=1, keepdims=True), (1, 128))
    q_span, q_mine = pl.ds(Q_AT, Q_ROWS), q_out.at[z * 2 + xh]
    q_out[z * 2 + xh] = src[z, Q_AT:]
    for dz in (1, 3, 2, 0):
        for dx in (1, 0):
            if dz or dx:
                start(src.at[zs[dz], q_span], q_mine, qr.at[dz * 2 + dx], (zs[dz], y, 1 - xh if dx else xh, c, hd))
    for s in range(1, 4):
        for p in range(2):
            first_hop(s, p)
            second_hop(s - 1, p)
            if s > 1:
                last_hop(s - 2, p)
    for p in range(2):
        second_hop(3, p)
        last_hop(2, p)
    for p in range(2):
        last_hop(3, p)

    for dz in range(4):
        for dx in range(2):
            if dz or dx:
                landed(q_out.at[zs[(4 - dz) % 4] * 2 + (1 - xh if dx else xh)], qr.at[dz * 2 + dx])
    for s in range(4):
        for i, yy in enumerate((y, down, up, over)):
            for p in range(2):
                landed(piece(came[s], yy, 1 - c, p), dd.at[s, i, p])
    for copy in sent:
        copy.wait_send()


def attend_kernel(kv, q, start_ref, o_ref, l_ref, plan, sm, low_s, bias_s, top_s, weight_s, acc_s, s_even, s_odd, sem):
    lane = lax.broadcasted_iota(jnp.int32, (1, 128), 1)
    lane32 = lax.broadcasted_iota(jnp.int32, (32, 128), 1)
    lane16 = lax.broadcasted_iota(jnp.int32, (16, 128), 1)
    code = lax.broadcasted_iota(jnp.int32, (32, 128), 0) * 2
    first = kv[:, 2 * GROUP, :].astype(jnp.float32).astype(jnp.int32)
    second = GROUPS - 1 - first
    at = jnp.where(first == lane32, code + 1, 0) + jnp.where(second == lane32, code + 2, 0)
    inv = jnp.sum(at, axis=0, keepdims=True) - 1
    here = jnp.where(inv >= 0, 1, 0)
    rank0 = jnp.sum(jnp.where(lane32 < first, here, 0), axis=1, keepdims=True)
    rank1 = jnp.sum(jnp.where(lane32 < second, here, 0), axis=1, keepdims=True)
    listed = jnp.where(rank0 == lane32, code * GROUPS, 0) + jnp.where(rank1 == lane32, (code + 1) * GROUPS, 0)
    plan[0:1, :] = jnp.sum(listed, axis=0, keepdims=True)
    plan[1:2, :] = inv

    q_first = q[:, 2 * GROUP, :].astype(jnp.float32).astype(jnp.int32)
    group = jnp.concatenate([q_first, GROUPS - 1 - q_first], axis=0)
    q_pos = group * GROUP + lane16
    low, low_first = jnp.zeros_like(q_pos), jnp.zeros_like(q_pos)
    for d in range(1, 16):
        begin = start_ref[d : d + 1, :]
        low = jnp.where(begin <= q_pos, begin, low)
        low_first = jnp.where(begin <= group * GROUP, begin, low_first)
    low_s[...] = low
    bias_s[...] = jnp.where(low == low_first, 0.0, MASKED)
    low_group = lax.shift_right_logical(low_first, 7)
    plan[16:32, :] = group
    plan[32:48, :] = low_group
    begin_at = jnp.sum(jnp.where(lane16 <= low_group, here, 0), axis=1, keepdims=True)
    end_at = jnp.sum(jnp.where(lane16 < group, here, 0), axis=1, keepdims=True)
    tiles = lax.shift_right_logical(jnp.maximum(end_at - begin_at, 0) + (TILE - 1), 2)
    begin_at, end_at, tiles = (jnp.broadcast_to(x, (16, 128)) for x in (begin_at, end_at, tiles))
    done = jnp.zeros((1, 128), jnp.int32)
    item = [lane, lane + 128, lane + 256]
    item_u, item_at, item_end = [[jnp.zeros((1, 128), jnp.int32) for _ in item] for _ in range(3)]
    for u in range(16):
        after = done + tiles[u : u + 1, :]
        for i, n in enumerate(item):
            mine = (done <= n) & (n < after)
            item_u[i] = jnp.where(mine, u, item_u[i])
            item_at[i] = jnp.where(mine, begin_at[u : u + 1, :] + (n - done) * TILE, item_at[i])
            item_end[i] = jnp.where(mine, end_at[u : u + 1, :], item_end[i])
        done = after
    for i in range(3):
        plan[2 + i : 3 + i, :] = item_u[i]
        plan[5 + i : 6 + i, :] = item_at[i]
        plan[8 + i : 9 + i, :] = item_end[i]
    plan[11:12, :] = done
    copy = pltpu.make_async_copy(plan, sm, sem)
    copy.start()
    copy.wait()

    row = lax.broadcasted_iota(jnp.int32, (GROUP, GROUP), 0)

    def half(slot, base):
        return pl.ds(pl.multiple_of(base + lax.rem(slot, 2) * GROUP, 16), GROUP)

    def queries_of(u):
        return q[lax.rem(u, 8), pl.ds(pl.multiple_of(lax.div(u, 8) * GROUP, GROUP), GROUP), :]

    def edges(u):
        g, low_g = sm[16 + u, 0], sm[32 + u, 0]
        q_t = queries_of(u)
        lower = low_s[pl.ds(u, 1), :]
        upper = g * GROUP + lane
        scores, held = [], []
        for key_group, wanted in ((g, True), (low_g, low_g < g)):
            found = sm[1, key_group]
            slot = jnp.maximum(found, 0)
            base = jnp.where((found >= 0) & wanted, key_group * GROUP, FAR)
            one = jnp.dot(kv[lax.div(slot, 2), half(slot, 0), :], q_t, preferred_element_type=jnp.float32)
            seen = (row >= lower - base) & (row <= upper - base)
            scores.append(jnp.where(seen, one, MASKED))
            held.append(kv[lax.div(slot, 2), half(slot, K_ROWS), :])
        top = jnp.full((1, GROUP), NEG, jnp.float32)
        for one in scores:
            top = jnp.maximum(top, jnp.max(one, axis=0, keepdims=True))
        parts = [jnp.exp2((one - top) * COEF) for one in scores]
        top_s[pl.ds(u, 1), :] = top
        weight_s[pl.ds(u, 1), :] = sum(jnp.sum(part, axis=0, keepdims=True) for part in parts)
        acc_s[u] = jnp.dot(
            jnp.concatenate(held, axis=1),
            jnp.concatenate([part.astype(jnp.bfloat16) for part in parts], axis=0),
            preferred_element_type=jnp.float32,
        )

    @pl.loop(0, 4)
    def _(k):
        for n in range(4):
            edges(4 * k + n)

    def read(i):
        r, k = lax.shift_right_logical(i, 7), lax.bitwise_and(i, 127)
        return sm[2 + r, k], sm[5 + r, k], sm[8 + r, k]

    def slot_of(e, end):
        return lax.shift_right_logical(sm[0, jnp.maximum(jnp.minimum(e, end - 1), 0)], 7)

    def score(i, dst):
        u, e, end = read(i)
        q_t = queries_of(u)
        for j in range(TILE):
            slot = slot_of(e + j, end)
            dst[j * GROUP : (j + 1) * GROUP, :] = jnp.dot(
                kv[lax.div(slot, 2), half(slot, 0), :], q_t, preferred_element_type=jnp.float32
            )

    def absorb(i, src):
        u, e, end = read(i)
        lanes = bias_s[pl.ds(u, 1), :]
        top = top_s[pl.ds(u, 1), :]
        new_top, biases, held, parts = top, [], [], []
        for j in range(TILE):
            biases.append(jnp.where(e + j < end, lanes, MASKED))
            best = jnp.max(src[j * GROUP : (j + 1) * GROUP, :], axis=0, keepdims=True)
            new_top = jnp.maximum(new_top, best + biases[j])
        factor = jnp.exp2((top - new_top) * COEF)
        weight = weight_s[pl.ds(u, 1), :] * factor
        for j in range(TILE):
            part = jnp.exp2((src[j * GROUP : (j + 1) * GROUP, :] - (new_top - biases[j])) * COEF)
            weight = weight + jnp.sum(part, axis=0, keepdims=True)
            parts.append(part.astype(jnp.bfloat16))
            slot = slot_of(e + j, end)
            held.append(kv[lax.div(slot, 2), half(slot, K_ROWS), :])
        top_s[pl.ds(u, 1), :] = new_top
        weight_s[pl.ds(u, 1), :] = weight
        acc_s[u] = acc_s[u] * factor + jnp.dot(
            jnp.concatenate(held, axis=1), jnp.concatenate(parts, axis=0), preferred_element_type=jnp.float32
        )

    total = sm[11, 0]
    score(jnp.int32(0), s_even)

    @pl.loop(0, lax.shift_right_logical(total + 7, 3))
    def _(k):
        for n in range(0, 8, 2):
            i = 8 * k + n
            score(i + 1, s_odd)
            absorb(i, s_even)
            score(i + 2, s_even)
            absorb(i + 1, s_odd)

    @pl.loop(0, 16, unroll=4)
    def _(u):
        weight = weight_s[pl.ds(u, 1), :]
        some = weight > 0.0
        safe = jnp.where(some, weight, 1.0)
        ch, s = lax.rem(u, 8), lax.div(u, 8)
        o_ref[ch, pl.ds(pl.multiple_of(s * GROUP, GROUP), GROUP), :] = (acc_s[u] * (1.0 / safe)).astype(jnp.bfloat16)
        l_ref[ch, pl.ds(s, 1), :] = jnp.where(some, top_s[pl.ds(u, 1), :] * COEF + jnp.log2(safe), NEG)


def merge_kernel(o_ref, l_ref, out_ref, o_in, l_in, snd, orecv, lrecv):
    z, y, xh, c, hd = place()
    zs = [z, lax.rem(z + 1, 4), lax.rem(z + 2, 4), lax.rem(z + 3, 4)]
    peers = [(dz, dx) for dz in (2, 1, 3, 0) for dx in (1, 0) if dz or dx]
    barrier = pltpu.get_barrier_semaphore()
    for dz, dx in peers:
        to = (zs[dz], y, 1 - xh if dx else xh, c, hd)
        pl.semaphore_signal(barrier, inc=1, device_id=to, device_id_type=MESH)
    mine = z * 2 + xh
    o_in[mine] = o_ref[mine]
    l_in[mine] = l_ref[mine]
    pl.semaphore_wait(barrier, len(peers))
    sent = []
    for n, (dz, dx) in enumerate(peers):
        side = 1 - xh if dx else xh
        to, theirs = (zs[dz], y, side, c, hd), zs[dz] * 2 + side
        for src, dst, recv in ((o_ref, o_in, orecv), (l_ref, l_in, lrecv)):
            copy = remote(src.at[theirs], dst.at[mine], snd.at[len(sent)], recv.at[dz * 2 + dx], to)
            copy.start()
            sent.append(copy)
    for dz, dx in peers:
        side = 1 - xh if dx else xh
        theirs = zs[(4 - dz) % 4] * 2 + side
        to = (zs[1], y, xh, c, hd)
        remote(o_ref.at[0], o_in.at[theirs], snd.at[0], orecv.at[dz * 2 + dx], to).wait_recv()
        remote(l_ref.at[0], l_in.at[theirs], snd.at[0], lrecv.at[dz * 2 + dx], to).wait_recv()
    for h in range(4):
        for s in range(2):
            rows = slice(s * GROUP, (s + 1) * GROUP)
            a, b = l_in[2 * h, s : s + 1, :], l_in[2 * h + 1, s : s + 1, :]
            most = jnp.maximum(a, b)
            wa, wb = jnp.exp2(a - most), jnp.exp2(b - most)
            total = wa + wb
            merged = o_in[2 * h, rows, :].astype(jnp.float32) * (wa / total)
            merged = merged + o_in[2 * h + 1, rows, :].astype(jnp.float32) * (wb / total)
            out_ref[rows, h * HEAD_DIM : (h + 1) * HEAD_DIM] = merged.T.astype(jnp.bfloat16)
    for copy in sent:
        copy.wait_send()


def shards(queries, keys, values, group_table, doc_ids):
    vmem = pl.BlockSpec(memory_space=pltpu.VMEM)
    hbm = pl.BlockSpec(memory_space=pltpu.HBM)
    dma = pltpu.SemaphoreType.DMA
    kv, q, begins = pl.pallas_call(
        spread_kernel,
        out_shape=(
            pltpu.VMEM((32, CHUNK, HEAD_DIM), jnp.bfloat16),
            pltpu.VMEM((8, Q_ROWS, HEAD_DIM), jnp.bfloat16),
            pltpu.VMEM((16, 128), jnp.int32),
        ),
        in_specs=[hbm] * 5,
        out_specs=(vmem, vmem, vmem),
        scratch_shapes=[
            pltpu.VMEM((4, Q_AT + Q_ROWS, HEAD_DIM), jnp.bfloat16),
            pltpu.VMEM(queries.shape, jnp.bfloat16),
            pltpu.VMEM(values.shape, jnp.bfloat16),
            pltpu.VMEM((128, 128), jnp.int32),
            pltpu.SMEM((1, 2), jnp.int32),
            dma((8,)), dma((69,)), dma((4, 2)), dma((4, 2)), dma((4, 2)), dma((4, 2)), dma((4, 4, 2)), dma((8,)),
        ],
        compiler_params=pltpu.CompilerParams(collective_id=0, has_side_effects=True, vmem_limit_bytes=62050000),
    )(queries, keys, values, group_table, doc_ids.reshape(128, 128))
    o, l = pl.pallas_call(
        attend_kernel,
        out_shape=(
            pltpu.VMEM((8, 2 * GROUP, HEAD_DIM), jnp.bfloat16),
            pltpu.VMEM((8, 8, GROUP), jnp.float32),
        ),
        in_specs=[vmem, vmem, vmem],
        out_specs=(vmem, vmem),
        scratch_shapes=[
            pltpu.VMEM((48, 128), jnp.int32),
            pltpu.SMEM((48, 128), jnp.int32),
            pltpu.VMEM((16, 128), jnp.int32),
            pltpu.VMEM((16, 128), jnp.float32),
            pltpu.VMEM((16, 128), jnp.float32),
            pltpu.VMEM((16, 128), jnp.float32),
            pltpu.VMEM((16, HEAD_DIM, GROUP), jnp.float32),
            pltpu.VMEM((TILE * GROUP, GROUP), jnp.float32),
            pltpu.VMEM((TILE * GROUP, GROUP), jnp.float32),
            dma,
        ],
        compiler_params=pltpu.CompilerParams(vmem_limit_bytes=16 << 20),
    )(kv, q, begins)
    return pl.pallas_call(
        merge_kernel,
        out_shape=jax.ShapeDtypeStruct(queries.shape, jnp.bfloat16),
        in_specs=[vmem, vmem],
        out_specs=vmem,
        scratch_shapes=[
            pltpu.VMEM((8, 2 * GROUP, HEAD_DIM), jnp.bfloat16),
            pltpu.VMEM((8, 8, GROUP), jnp.float32),
            dma((14,)), dma((8,)), dma((8,)),
        ],
        compiler_params=pltpu.CompilerParams(collective_id=1, has_side_effects=True, vmem_limit_bytes=16 << 20),
    )(o, l)


def solution(mesh):
    split = Mesh(mesh.devices.reshape(4, 4, 2, 2, mesh.shape["head"]), AXES)
    return jax.shard_map(
        shards,
        mesh=split,
        in_specs=(P(BLK, "head"), P(BLK, "head"), P(BLK, "head"), P(BLK, None), P()),
        out_specs=P(BLK, "head"),
        check_vma=False,
    )
```

profile of v0, /device:TPU:8, one launch (start us, length us, event | category | flops | bytes accessed | tf_op | source)
XLA Modules:
  0.0 57.9 jit_solution(3905010918803457665)
XLA Ops:
  0.0 30.9 %shard_map.55 = (bf16[32,528,128]{2,1,0:T(8,128)(2,1)S(1)}, bf16[8,272,128]{2,1,0:T(8,128)(2,1)S(1)}, s32[16,128]{1,0:T(8,128)S(1)}) custom-call(bf16[256,512]{1,0:T(8,128)(2,1)} %q_hbm.1, bf16[256,512]{1,0:T(8,128)(2,1)} %k_hbm.1, bf16[256,512]{1,0:T(8,128)(2,1)} %v_hbm.1, s32[1,2]{1,0:T(1,128)} %table_hbm.1, s32[128,128]{1,0:T(8,128)} %bitcast.1), custom_call_target="tpu_custom_call" | custom-call | tf_op jit(solution)/shard_map/pallas_call | solution.py:361
  30.9 10.2 %shard_map.56 = (bf16[8,256,128]{2,1,0:T(8,128)(2,1)S(1)}, f32[8,8,128]{2,1,0:T(8,128)S(1)}) custom-call(bf16[32,528,128]{2,1,0:T(8,128)(2,1)S(1)} %get-tuple-element.10.kv, bf16[8,272,128]{2,1,0:T(8,128)(2,1)S(1)} %get-tuple-element.11.q, s32[16,128]{1,0:T(8,128)S(1)} %get-tuple-element.12.start_ref), custom_call_target="tpu_custom_call" | custom-call | tf_op jit(solution)/shard_map/pallas_call | solution.py:380
  41.2 16.0 %shard_map.57 = bf16[256,512]{1,0:T(8,128)(2,1)S(1)} custom-call(bf16[8,256,128]{2,1,0:T(8,128)(2,1)S(1)} %get-tuple-element.13.o_ref, f32[8,8,128]{2,1,0:T(8,128)S(1)} %get-tuple-element.14.l_ref), custom_call_target="tpu_custom_call" | custom-call | tf_op jit(solution)/shard_map/pallas_call | solution.py:402
  57.2 0.7 %copy.7 = bf16[256,512]{1,0:T(8,128)(2,1)} copy(bf16[256,512]{1,0:T(8,128)(2,1)S(1)} %shard_map.57) | data formatting | bytes 524288
where the time goes:
time: 58.8 us; the launch traced here: 57.9 us
  Pallas kernels  57.1 us (97%)
  local copies, waits for them, and re-layouts  0.71 us (1%)
    pallas_call x1, Pallas kernels, shards(): pl.pallas_call(spread_kernel, out_shape=(pltpu.VMEM((32, CHUNK, HEAD_DIM)...  30.9 us
    pallas_call x1, Pallas kernels, shards(): pl.pallas_call(merge_kernel, out_shape=jax.ShapeDtypeStruct(queries.shape...  16 us
    pallas_call x1, Pallas kernels, shards(): pl.pallas_call(attend_kernel, out_shape=(pltpu.VMEM((8, 2 * GROUP, HEAD_D...  10.2 us

commit v1 on v0

--- a/solution.py
+++ b/solution.py
@@ -133,16 +133,20 @@
         start_out[d : d + 1, :] = jnp.broadcast_to(jnp.sum(counted, axis=1, keepdims=True), (1, 128))
     q_span, q_mine = pl.ds(Q_AT, Q_ROWS), q_out.at[z * 2 + xh]
     q_out[z * 2 + xh] = src[z, Q_AT:]
-    for dz in (1, 3, 2, 0):
-        for dx in (1, 0):
-            if dz or dx:
-                start(src.at[zs[dz], q_span], q_mine, qr.at[dz * 2 + dx], (zs[dz], y, 1 - xh if dx else xh, c, hd))
+    def send_queries():
+        for dz in (1, 3, 2, 0):
+            for dx in (1, 0):
+                if dz or dx:
+                    start(src.at[zs[dz], q_span], q_mine, qr.at[dz * 2 + dx], (zs[dz], y, 1 - xh if dx else xh, c, hd))
+
     for s in range(1, 4):
         for p in range(2):
             first_hop(s, p)
             second_hop(s - 1, p)
             if s > 1:
                 last_hop(s - 2, p)
+        if s == 2:
+            send_queries()
     for p in range(2):
         second_hop(3, p)
         last_hop(2, p)

time: 58.8 us -> 56 us (0.952)
  the two profiles are of different devices: /device:TPU:8 before, /device:TPU:1 now
where the time goes in v1:
time: 56 us; the launch traced here: 56.1 us
  Pallas kernels  55.3 us (99%)
  local copies, waits for them, and re-layouts  0.71 us (1%)
    pallas_call x1, Pallas kernels, shards(): pl.pallas_call(spread_kernel, out_shape=(pltpu.VMEM((32, CHUNK, HEAD_DIM)...  32.4 us
    pallas_call x1, Pallas kernels, shards(): pl.pallas_call(attend_kernel, out_shape=(pltpu.VMEM((8, 2 * GROUP, HEAD_D...  11.6 us
    pallas_call x1, Pallas kernels, shards(): pl.pallas_call(merge_kernel, out_shape=jax.ShapeDtypeStruct(queries.shape...  11.4 us

profile of v1, /device:TPU:1, one launch (start us, length us, event | category | flops | bytes accessed | tf_op | source)
XLA Modules:
  0.0 56.1 jit_solution(12348747891749055475)
XLA Ops:
  0.0 32.4 %shard_map.55 = (bf16[32,528,128]{2,1,0:T(8,128)(2,1)S(1)}, bf16[8,272,128]{2,1,0:T(8,128)(2,1)S(1)}, s32[16,128]{1,0:T(8,128)S(1)}) custom-call(bf16[256,512]{1,0:T(8,128)(2,1)} %q_hbm.1, bf16[256,512]{1,0:T(8,128)(2,1)} %k_hbm.1, bf16[256,512]{1,0:T(8,128)(2,1)} %v_hbm.1, s32[1,2]{1,0:T(1,128)} %table_hbm.1, s32[128,128]{1,0:T(8,128)} %bitcast.1), custom_call_target="tpu_custom_call" | custom-call | tf_op jit(solution)/shard_map/pallas_call | solution.py:365
  32.4 11.6 %shard_map.56 = (bf16[8,256,128]{2,1,0:T(8,128)(2,1)S(1)}, f32[8,8,128]{2,1,0:T(8,128)S(1)}) custom-call(bf16[32,528,128]{2,1,0:T(8,128)(2,1)S(1)} %get-tuple-element.10.kv, bf16[8,272,128]{2,1,0:T(8,128)(2,1)S(1)} %get-tuple-element.11.q, s32[16,128]{1,0:T(8,128)S(1)} %get-tuple-element.12.start_ref), custom_call_target="tpu_custom_call" | custom-call | tf_op jit(solution)/shard_map/pallas_call | solution.py:384
  43.9 11.4 %shard_map.57 = bf16[256,512]{1,0:T(8,128)(2,1)S(1)} custom-call(bf16[8,256,128]{2,1,0:T(8,128)(2,1)S(1)} %get-tuple-element.13.o_ref, f32[8,8,128]{2,1,0:T(8,128)S(1)} %get-tuple-element.14.l_ref), custom_call_target="tpu_custom_call" | custom-call | tf_op jit(solution)/shard_map/pallas_call | solution.py:406
  55.4 0.7 %copy.7 = bf16[256,512]{1,0:T(8,128)(2,1)} copy(bf16[256,512]{1,0:T(8,128)(2,1)S(1)} %shard_map.57) | data formatting | bytes 524288

commit v2 on v1

--- a/solution.py
+++ b/solution.py
@@ -103,14 +103,12 @@
 
     def second_hop(s, p):
         below, above = piece(came[s], down, c, p), piece(came[s], up, c, p)
-        landed(below, yp.at[s, p])
-        if p == 0:
-            start(below, below, rl.at[s, p], to_up)
-        start(below, below, dd.at[s, 1, p], to_core)
-        landed(above, ym.at[s, p])
-        if p == 1:
-            start(above, above, rl.at[s, p], to_down)
-        start(above, above, dd.at[s, 2, p], to_core)
+        ways = [(below, yp, to_up, 1), (above, ym, to_down, 2)]
+        for ref, came_in, onward, i in ways if p == 0 else ways[::-1]:
+            landed(ref, came_in.at[s, p])
+            if i == 1 + p:
+                start(ref, ref, rl.at[s, p], onward)
+            start(ref, ref, dd.at[s, i, p], to_core)
 
     def last_hop(s, p):
         across = piece(came[s], over, c, p)
@@ -252,10 +250,10 @@
             preferred_element_type=jnp.float32,
         )
 
-    @pl.loop(0, 4)
+    @pl.loop(0, 2)
     def _(k):
-        for n in range(4):
-            edges(4 * k + n)
+        for n in range(8):
+            edges(8 * k + n)
 
     def read(i):
         r, k = lax.shift_right_logical(i, 7), lax.bitwise_and(i, 127)

time: 56 us -> 54.8 us (0.979)
  the two profiles are of different devices: /device:TPU:1 before, /device:TPU:16 now
where the time goes in v2:
time: 54.8 us; the launch traced here: 54.9 us
  Pallas kernels  54.2 us (99%)
  local copies, waits for them, and re-layouts  0.71 us (1%)
    pallas_call x1, Pallas kernels, shards(): pl.pallas_call(spread_kernel, out_shape=(pltpu.VMEM((32, CHUNK, HEAD_DIM)...  29.8 us
    pallas_call x1, Pallas kernels, shards(): pl.pallas_call(merge_kernel, out_shape=jax.ShapeDtypeStruct(queries.shape...  13.4 us
    pallas_call x1, Pallas kernels, shards(): pl.pallas_call(attend_kernel, out_shape=(pltpu.VMEM((8, 2 * GROUP, HEAD_D...  11 us

profile of v2, /device:TPU:16, one launch (start us, length us, event | category | flops | bytes accessed | tf_op | source)
XLA Modules:
  0.0 54.9 jit_solution(725141861822615817)
XLA Ops:
  0.0 29.8 %shard_map.55 = (bf16[32,528,128]{2,1,0:T(8,128)(2,1)S(1)}, bf16[8,272,128]{2,1,0:T(8,128)(2,1)S(1)}, s32[16,128]{1,0:T(8,128)S(1)}) custom-call(bf16[256,512]{1,0:T(8,128)(2,1)} %q_hbm.1, bf16[256,512]{1,0:T(8,128)(2,1)} %k_hbm.1, bf16[256,512]{1,0:T(8,128)(2,1)} %v_hbm.1, s32[1,2]{1,0:T(1,128)} %table_hbm.1, s32[128,128]{1,0:T(8,128)} %bitcast.1), custom_call_target="tpu_custom_call" | custom-call | tf_op jit(solution)/shard_map/pallas_call | solution.py:363
  29.8 11.0 %shard_map.56 = (bf16[8,256,128]{2,1,0:T(8,128)(2,1)S(1)}, f32[8,8,128]{2,1,0:T(8,128)S(1)}) custom-call(bf16[32,528,128]{2,1,0:T(8,128)(2,1)S(1)} %get-tuple-element.10.kv, bf16[8,272,128]{2,1,0:T(8,128)(2,1)S(1)} %get-tuple-element.11.q, s32[16,128]{1,0:T(8,128)S(1)} %get-tuple-element.12.start_ref), custom_call_target="tpu_custom_call" | custom-call | tf_op jit(solution)/shard_map/pallas_call | solution.py:382
  40.8 13.4 %shard_map.57 = bf16[256,512]{1,0:T(8,128)(2,1)S(1)} custom-call(bf16[8,256,128]{2,1,0:T(8,128)(2,1)S(1)} %get-tuple-element.13.o_ref, f32[8,8,128]{2,1,0:T(8,128)S(1)} %get-tuple-element.14.l_ref), custom_call_target="tpu_custom_call" | custom-call | tf_op jit(solution)/shard_map/pallas_call | solution.py:404
  54.2 0.7 %copy.7 = bf16[256,512]{1,0:T(8,128)(2,1)} copy(bf16[256,512]{1,0:T(8,128)(2,1)S(1)} %shard_map.57) | data formatting | bytes 524288

commit v3 on v2

--- a/solution.py
+++ b/solution.py
@@ -297,14 +297,23 @@
     total = sm[11, 0]
     score(jnp.int32(0), s_even)
 
-    @pl.loop(0, lax.shift_right_logical(total + 7, 3))
-    def _(k):
-        for n in range(0, 8, 2):
-            i = 8 * k + n
+    def run(first, count):
+        for n in range(0, count, 2):
+            i = first + n
             score(i + 1, s_odd)
             absorb(i, s_even)
             score(i + 2, s_even)
             absorb(i + 1, s_odd)
+
+    eights = lax.shift_right_logical(total + 3, 3)
+
+    @pl.loop(0, eights)
+    def _(k):
+        run(8 * k, 8)
+
+    @pl.loop(0, lax.shift_right_logical(jnp.maximum(total - 8 * eights, 0) + 3, 2))
+    def _(k):
+        run(8 * eights + 4 * k, 4)
 
     @pl.loop(0, 16, unroll=4)
     def _(u):

time: 54.8 us -> 55.2 us (level)
  the two profiles are of different devices: /device:TPU:16 before, /device:TPU:17 now
where the time goes in v3:
time: 55.2 us; the launch traced here: 54.8 us
  Pallas kernels  54.1 us (98%)
  local copies, waits for them, and re-layouts  0.71 us (1%)
    pallas_call x1, Pallas kernels, shards(): pl.pallas_call(spread_kernel, out_shape=(pltpu.VMEM((32, CHUNK, HEAD_DIM)...  30.4 us
    pallas_call x1, Pallas kernels, shards(): pl.pallas_call(attend_kernel, out_shape=(pltpu.VMEM((8, 2 * GROUP, HEAD_D...  12.3 us
    pallas_call x1, Pallas kernels, shards(): pl.pallas_call(merge_kernel, out_shape=jax.ShapeDtypeStruct(queries.shape...  11.3 us

profile of v3, /device:TPU:17, one launch (start us, length us, event | category | flops | bytes accessed | tf_op | source)
XLA Modules:
  0.0 54.8 jit_solution(8659813748177277129)
XLA Ops:
  0.0 30.4 %shard_map.55 = (bf16[32,528,128]{2,1,0:T(8,128)(2,1)S(1)}, bf16[8,272,128]{2,1,0:T(8,128)(2,1)S(1)}, s32[16,128]{1,0:T(8,128)S(1)}) custom-call(bf16[256,512]{1,0:T(8,128)(2,1)} %q_hbm.1, bf16[256,512]{1,0:T(8,128)(2,1)} %k_hbm.1, bf16[256,512]{1,0:T(8,128)(2,1)} %v_hbm.1, s32[1,2]{1,0:T(1,128)} %table_hbm.1, s32[128,128]{1,0:T(8,128)} %bitcast.1), custom_call_target="tpu_custom_call" | custom-call | tf_op jit(solution)/shard_map/pallas_call | solution.py:372
  30.5 12.3 %shard_map.56 = (bf16[8,256,128]{2,1,0:T(8,128)(2,1)S(1)}, f32[8,8,128]{2,1,0:T(8,128)S(1)}) custom-call(bf16[32,528,128]{2,1,0:T(8,128)(2,1)S(1)} %get-tuple-element.10.kv, bf16[8,272,128]{2,1,0:T(8,128)(2,1)S(1)} %get-tuple-element.11.q, s32[16,128]{1,0:T(8,128)S(1)} %get-tuple-element.12.start_ref), custom_call_target="tpu_custom_call" | custom-call | tf_op jit(solution)/shard_map/pallas_call | solution.py:391
  42.8 11.3 %shard_map.57 = bf16[256,512]{1,0:T(8,128)(2,1)S(1)} custom-call(bf16[8,256,128]{2,1,0:T(8,128)(2,1)S(1)} %get-tuple-element.13.o_ref, f32[8,8,128]{2,1,0:T(8,128)S(1)} %get-tuple-element.14.l_ref), custom_call_target="tpu_custom_call" | custom-call | tf_op jit(solution)/shard_map/pallas_call | solution.py:413
  54.1 0.7 %copy.7 = bf16[256,512]{1,0:T(8,128)(2,1)} copy(bf16[256,512]{1,0:T(8,128)(2,1)S(1)} %shard_map.57) | data formatting | bytes 524288

commit v4 on v3

--- a/solution.py
+++ b/solution.py
@@ -305,15 +305,15 @@
             score(i + 2, s_even)
             absorb(i + 1, s_odd)
 
-    eights = lax.shift_right_logical(total + 3, 3)
-
-    @pl.loop(0, eights)
+    sixteens = lax.shift_right_logical(total + 3, 4)
+
+    @pl.loop(0, sixteens)
     def _(k):
-        run(8 * k, 8)
-
-    @pl.loop(0, lax.shift_right_logical(jnp.maximum(total - 8 * eights, 0) + 3, 2))
+        run(16 * k, 16)
+
+    @pl.loop(0, lax.shift_right_logical(jnp.maximum(total - 16 * sixteens, 0) + 3, 2))
     def _(k):
-        run(8 * eights + 4 * k, 4)
+        run(16 * sixteens + 4 * k, 4)
 
     @pl.loop(0, 16, unroll=4)
     def _(u):
@@ -334,8 +334,6 @@
         to = (zs[dz], y, 1 - xh if dx else xh, c, hd)
         pl.semaphore_signal(barrier, inc=1, device_id=to, device_id_type=MESH)
     mine = z * 2 + xh
-    o_in[mine] = o_ref[mine]
-    l_in[mine] = l_ref[mine]
     pl.semaphore_wait(barrier, len(peers))
     sent = []
     for n, (dz, dx) in enumerate(peers):
@@ -345,6 +343,8 @@
             copy = remote(src.at[theirs], dst.at[mine], snd.at[len(sent)], recv.at[dz * 2 + dx], to)
             copy.start()
             sent.append(copy)
+    o_in[mine] = o_ref[mine]
+    l_in[mine] = l_ref[mine]
     for dz, dx in peers:
         side = 1 - xh if dx else xh
         theirs = zs[(4 - dz) % 4] * 2 + side

time: 55.2 us -> 54.6 us (0.989)
  the two profiles are of different devices: /device:TPU:17 before, /device:TPU:16 now
where the time goes in v4:
time: 54.6 us; the launch traced here: 54.8 us
  Pallas kernels  54 us (99%)
  local copies, waits for them, and re-layouts  0.71 us (1%)
    pallas_call x1, Pallas kernels, shards(): pl.pallas_call(spread_kernel, out_shape=(pltpu.VMEM((32, CHUNK, HEAD_DIM)...  29.8 us
    pallas_call x1, Pallas kernels, shards(): pl.pallas_call(merge_kernel, out_shape=jax.ShapeDtypeStruct(queries.shape...  14.1 us
    pallas_call x1, Pallas kernels, shards(): pl.pallas_call(attend_kernel, out_shape=(pltpu.VMEM((8, 2 * GROUP, HEAD_D...  10.1 us

profile of v4, /device:TPU:16, one launch (start us, length us, event | category | flops | bytes accessed | tf_op | source)
XLA Modules:
  0.0 54.8 jit_solution(6166139848580478796)
XLA Ops:
  0.0 29.8 %shard_map.55 = (bf16[32,528,128]{2,1,0:T(8,128)(2,1)S(1)}, bf16[8,272,128]{2,1,0:T(8,128)(2,1)S(1)}, s32[16,128]{1,0:T(8,128)S(1)}) custom-call(bf16[256,512]{1,0:T(8,128)(2,1)} %q_hbm.1, bf16[256,512]{1,0:T(8,128)(2,1)} %k_hbm.1, bf16[256,512]{1,0:T(8,128)(2,1)} %v_hbm.1, s32[1,2]{1,0:T(1,128)} %table_hbm.1, s32[128,128]{1,0:T(8,128)} %bitcast.1), custom_call_target="tpu_custom_call" | custom-call | tf_op jit(solution)/shard_map/pallas_call | solution.py:372
  29.8 10.1 %shard_map.56 = (bf16[8,256,128]{2,1,0:T(8,128)(2,1)S(1)}, f32[8,8,128]{2,1,0:T(8,128)S(1)}) custom-call(bf16[32,528,128]{2,1,0:T(8,128)(2,1)S(1)} %get-tuple-element.10.kv, bf16[8,272,128]{2,1,0:T(8,128)(2,1)S(1)} %get-tuple-element.11.q, s32[16,128]{1,0:T(8,128)S(1)} %get-tuple-element.12.start_ref), custom_call_target="tpu_custom_call" | custom-call | tf_op jit(solution)/shard_map/pallas_call | solution.py:391
  39.9 14.1 %shard_map.57 = bf16[256,512]{1,0:T(8,128)(2,1)S(1)} custom-call(bf16[8,256,128]{2,1,0:T(8,128)(2,1)S(1)} %get-tuple-element.13.o_ref, f32[8,8,128]{2,1,0:T(8,128)S(1)} %get-tuple-element.14.l_ref), custom_call_target="tpu_custom_call" | custom-call | tf_op jit(solution)/shard_map/pallas_call | solution.py:413
  54.1 0.7 %copy.7 = bf16[256,512]{1,0:T(8,128)(2,1)} copy(bf16[256,512]{1,0:T(8,128)(2,1)S(1)} %shard_map.57) | data formatting | bytes 524288
